TPU v7x, 32 devices: a whole 2x2x4 slice. The times are simulated.
32 devices in a mesh: dp: 8 (over z, y), tensor: 4 (over x, core).
Axes of the slice: x: 2, y: 2, z: 4, core: 2. Of those that a mesh axis runs over, the one named last changes fastest.
Arguments:
- acts: bfloat16 [8, 2048, 1024], P('dp', 'tensor'), may hold values from -6 to 6
- grad_out: bfloat16 [8, 2048, 1024], P('dp', 'tensor'), may hold values from -6 to 6
- norm_gain: float32 [1024], replicated, may hold values from 0.5 to 1.5
- w_zx: bfloat16 [1024, 2, 2048], P('dp', None, 'tensor'), may hold values from -0.1875 to 0.1875
- w_bc: bfloat16 [1024, 256], P('dp'), may hold values from -0.1875 to 0.1875
- w_dt: bfloat16 [1024, 32], P('dp', 'tensor'), may hold values from -0.1875 to 0.1875
- w_out: bfloat16 [1024, 2048], P('dp', 'tensor'), may hold values from -0.125 to 0.125
- conv_x: float32 [4, 2048], replicated, may hold values from -3 to 3
- conv_x_bias: float32 [2048], replicated, may hold values from -0.5 to 0.5
- conv_bc: float32 [4, 256], replicated, may hold values from -3 to 3
- conv_bc_bias: float32 [256], replicated, may hold values from -0.5 to 0.5
- dt_bias: float32 [32], replicated, may hold values from -7 to -2
- a_log: float32 [32], replicated, may hold values from 0 to 2.77
- d_skip: float32 [32], replicated, may hold values from 0.5 to 1.5
- gate_gain: float32 [2048], replicated, may hold values from 0.5 to 1.5
Outputs:
- out_acts: bfloat16 [8, 2048, 1024], P('dp', 'tensor')
- grad_acts: float32 [8, 2048, 1024], P('dp', 'tensor')
- grad_norm_gain: float32 [1024], replicated
- grad_w_zx: float32 [1024, 2, 2048], P('dp', None, 'tensor')
- grad_w_bc: float32 [1024, 256], P('dp')
- grad_w_dt: float32 [1024, 32], P('dp', 'tensor')
- grad_w_out: float32 [1024, 2048], P('dp', 'tensor')
- grad_conv_x: float32 [4, 2048], replicated
- grad_conv_x_bias: float32 [2048], replicated
- grad_conv_bc: float32 [4, 256], replicated
- grad_conv_bc_bias: float32 [256], replicated
- grad_dt_bias: float32 [32], replicated
- grad_a_log: float32 [32], replicated
- grad_d_skip: float32 [32], replicated
- grad_gate_gain: float32 [2048], replicated
All inputs are finite; a program needn't handle non-finite values.
Results may differ from a plain program's by a relative error of at most 0.0096.
Values may be sent and summed in bfloat16 or wider, within the bound.
A program may use at most 192 MiB of HBM per device.

v0:
```python
import jax
import jax.numpy as jnp
from jax import lax
from jax.sharding import PartitionSpec as P

BLOCK_LEN = 256
EPSILON = 1e-05
FULL_PRECISION = lax.Precision.HIGHEST
CONTRACT_LAST = (((1,), (1,)), ((), ()))
CONTRACT_FIRST = (((0,), (0,)), ((), ()))


def causal_conv(values, conv_taps):
    tap_count = conv_taps.shape[0]
    length = values.shape[0]
    padded = jnp.pad(values, ((tap_count - 1, 0), (0, 0)))
    result = conv_taps[0] * padded[0:length]
    for offset in range(1, tap_count):
        result = result + conv_taps[offset] * padded[offset : offset + length]
    return result


def ssd_scan(x_heads, step_dt, decay_rate, b_mat, c_mat, block_size):
    length, head_count, head_width = x_heads.shape
    state_count = b_mat.shape[1]
    block_count = length // block_size
    x_blocks = x_heads.reshape(block_count, block_size, head_count, head_width)
    dt_blocks = step_dt.reshape(block_count, block_size, head_count)
    b_blocks = b_mat.reshape(block_count, block_size, state_count)
    c_blocks = c_mat.reshape(block_count, block_size, state_count)
    positions = jnp.arange(block_size)
    causal_mask = (positions[:, None] >= positions[None, :]).astype(jnp.float32)

    def step_block(state, inputs):
        x_block, dt_block, b_block, c_block = inputs
        cum_logs = jnp.cumsum(dt_block * decay_rate[None, :], axis=0)
        scores = jnp.dot(c_block, b_block.T, precision=FULL_PRECISION)
        log_gaps = (cum_logs[:, None, :] - cum_logs[None, :, :]) * causal_mask[:, :, None]
        weights = (
            scores[:, :, None] * jnp.exp(log_gaps) * causal_mask[:, :, None] * dt_block[None, :, :]
        )
        within = jnp.einsum("ijh,jhp->ihp", weights, x_block, precision=FULL_PRECISION)
        carried = (
            jnp.einsum("in,hpn->ihp", c_block, state, precision=FULL_PRECISION)
            * jnp.exp(cum_logs)[:, :, None]
        )
        block_total = cum_logs[-1]
        state_weight = jnp.exp(block_total[None, :] - cum_logs) * dt_block
        update = jnp.einsum(
            "jhp,jn->hpn", x_block * state_weight[:, :, None], b_block, precision=FULL_PRECISION
        )
        new_state = state * jnp.exp(block_total)[:, None, None] + update
        return (new_state, within + carried)

    zero_state = jnp.zeros((head_count, head_width, state_count), jnp.float32)
    final_state, outputs = lax.scan(
        jax.checkpoint(step_block), zero_state, (x_blocks, dt_blocks, b_blocks, c_blocks)
    )
    return outputs.reshape(length, head_count, head_width)


def pre_norm(acts_row, norm_gain):
    return (
        acts_row
        * lax.rsqrt(jnp.mean(acts_row * acts_row, axis=-1, keepdims=True) + EPSILON)
        * norm_gain
    )


def conv_part(x_vals, bc_vals, x_taps, x_shift, bc_taps, bc_shift):
    x_conv = jax.nn.silu(causal_conv(x_vals, x_taps) + x_shift)
    bc_conv = jax.nn.silu(causal_conv(bc_vals, bc_taps) + bc_shift)
    return (x_conv, bc_conv)


def mix_part(x_vals, b_vals, c_vals, dt_vals, dt_shift, log_rate, skip_gain, gate_vals):
    length = x_vals.shape[0]
    head_count = dt_vals.shape[1]
    x_heads = x_vals.reshape(length, head_count, -1)
    step_dt = jax.nn.softplus(dt_vals + dt_shift)
    mixed = (
        ssd_scan(x_heads, step_dt, -jnp.exp(log_rate), b_vals, c_vals, BLOCK_LEN)
        + skip_gain[None, :, None] * x_heads
    )
    return mixed.reshape(length, -1) * jax.nn.silu(gate_vals)


def widen(piece, start, full_size):
    holder = jnp.zeros(piece.shape[:-1] + (full_size,), jnp.float32)
    return lax.dynamic_update_slice_in_dim(holder, piece, start, piece.ndim - 1)


def body(
    acts,
    grad_out,
    norm_gain,
    w_zx,
    w_bc,
    w_dt,
    w_out,
    conv_x,
    conv_x_bias,
    conv_bc,
    conv_bc_bias,
    dt_bias,
    a_log,
    d_skip,
    gate_gain,
):
    parts = lax.axis_size("tensor")
    rank = lax.axis_index("tensor")
    local_rows = acts.shape[1]
    channels = w_zx.shape[2]
    head_count = w_dt.shape[1]
    state_count = w_bc.shape[1] // 2
    total_channels = channels * parts
    total_heads = head_count * parts
    chan_start = rank * channels
    head_start = rank * head_count
    zx_full, bc_full, dt_full, out_full = (
        lax.all_gather(w_zx, "dp", axis=0, tiled=True),
        lax.all_gather(w_bc, "dp", axis=0, tiled=True),
        lax.all_gather(w_dt, "dp", axis=0, tiled=True),
        lax.all_gather(w_out, "dp", axis=0, tiled=True),
    )
    acts_row = acts[0].astype(jnp.float32)
    normed_in, pre_back = jax.vjp(pre_norm, acts_row, norm_gain)
    hidden = lax.all_gather(normed_in.astype(jnp.bfloat16), "tensor", axis=0, tiled=True)
    zx_proj = jnp.einsum("ld,dkc->lkc", hidden, zx_full, preferred_element_type=jnp.float32)
    bc_proj = jnp.dot(hidden, bc_full, preferred_element_type=jnp.float32)
    dt_proj = jnp.dot(hidden, dt_full, preferred_element_type=jnp.float32)
    conv_x_local = lax.dynamic_slice_in_dim(conv_x, chan_start, channels, 1)
    conv_xb_local = lax.dynamic_slice_in_dim(conv_x_bias, chan_start, channels, 0)
    dt_bias_local = lax.dynamic_slice_in_dim(dt_bias, head_start, head_count, 0)
    a_log_local = lax.dynamic_slice_in_dim(a_log, head_start, head_count, 0)
    d_skip_local = lax.dynamic_slice_in_dim(d_skip, head_start, head_count, 0)
    gain_local = lax.dynamic_slice_in_dim(gate_gain, chan_start, channels, 0)
    conv_outs, conv_back = jax.vjp(
        conv_part, zx_proj[:, 1], bc_proj, conv_x_local, conv_xb_local, conv_bc, conv_bc_bias
    )
    x_conv, bc_conv = conv_outs
    x_low = x_conv.astype(jnp.bfloat16)
    b_low = bc_conv[:, :state_count].astype(jnp.bfloat16)
    c_low = bc_conv[:, state_count:].astype(jnp.bfloat16)
    gated, mix_back = jax.vjp(
        mix_part,
        x_low.astype(jnp.float32),
        b_low.astype(jnp.float32),
        c_low.astype(jnp.float32),
        dt_proj,
        dt_bias_local,
        a_log_local,
        d_skip_local,
        zx_proj[:, 0],
    )
    square_total = lax.psum(jnp.sum(gated * gated, axis=1), "tensor")
    inv_rms = lax.rsqrt(square_total / total_channels + EPSILON)[:, None]
    mixed_out = (gated * inv_rms * gain_local).astype(jnp.bfloat16)
    projected = lax.psum_scatter(
        lax.dot_general(mixed_out, out_full, CONTRACT_LAST, preferred_element_type=jnp.float32),
        "tensor",
        scatter_dimension=0,
        tiled=True,
    )
    out_acts = (acts_row + projected).astype(jnp.bfloat16)[None]
    grad_row = grad_out[0]
    grad_rows_all = lax.all_gather(grad_row, "tensor", axis=0, tiled=True)
    grad_mixed = jnp.dot(grad_rows_all, out_full, preferred_element_type=jnp.float32).astype(
        jnp.bfloat16
    )
    grad_out_w = lax.dot_general(
        grad_rows_all, mixed_out, CONTRACT_FIRST, preferred_element_type=jnp.float32
    )
    grad_normed = grad_mixed.astype(jnp.float32)
    grad_gain_local = jnp.sum(grad_normed * gated * inv_rms, axis=0)
    scaled = grad_normed * gain_local
    row_dot = lax.psum(jnp.sum(scaled * gated, axis=1), "tensor")
    grad_gated = (
        inv_rms * scaled
        - gated * (inv_rms * inv_rms * inv_rms) * (row_dot / total_channels)[:, None]
    )
    (
        grad_x_low,
        grad_b,
        grad_c,
        grad_dt_in,
        grad_dt_shift,
        grad_log_rate,
        grad_skip,
        grad_gate_in,
    ) = mix_back(grad_gated)
    grad_x_in, grad_bc_part, grad_x_taps, grad_x_shift, grad_bc_taps, grad_bc_shift = conv_back(
        (grad_x_low, jnp.concatenate([grad_b, grad_c], axis=1))
    )
    grad_bc_in = lax.psum(grad_bc_part, "tensor").astype(jnp.bfloat16)
    grad_zx = jnp.stack([grad_gate_in.astype(jnp.bfloat16), grad_x_in.astype(jnp.bfloat16)], axis=1)
    grad_dt_low = grad_dt_in.astype(jnp.bfloat16)
    grad_zx_w = jnp.einsum("ld,lkc->dkc", hidden, grad_zx, preferred_element_type=jnp.float32)
    grad_bc_w = lax.dot_general(
        hidden, grad_bc_in, CONTRACT_FIRST, preferred_element_type=jnp.float32
    )
    grad_dt_w = lax.dot_general(
        hidden, grad_dt_low, CONTRACT_FIRST, preferred_element_type=jnp.float32
    )
    from_zx = jnp.einsum("lkc,dkc->ld", grad_zx, zx_full, preferred_element_type=jnp.float32)
    grad_hidden = lax.psum_scatter(
        from_zx
        + lax.dot_general(grad_dt_low, dt_full, CONTRACT_LAST, preferred_element_type=jnp.float32),
        "tensor",
        scatter_dimension=0,
        tiled=True,
    )
    bc_piece = lax.dynamic_slice_in_dim(grad_bc_in, rank * local_rows, local_rows, 0)
    grad_hidden = grad_hidden + lax.dot_general(
        bc_piece, bc_full, CONTRACT_LAST, preferred_element_type=jnp.float32
    )
    grad_acts_norm, grad_norm_gain = pre_back(grad_hidden)
    grad_acts = (grad_row.astype(jnp.float32) + grad_acts_norm)[None]
    grad_w_zx, grad_w_bc, grad_w_dt, grad_w_out = (
        lax.psum_scatter(grad_zx_w, "dp", scatter_dimension=0, tiled=True),
        lax.psum_scatter(grad_bc_w, "dp", scatter_dimension=0, tiled=True),
        lax.psum_scatter(grad_dt_w, "dp", scatter_dimension=0, tiled=True),
        lax.psum_scatter(grad_out_w, "dp", scatter_dimension=0, tiled=True),
    )
    small_sums = lax.psum(
        (
            grad_norm_gain,
            widen(grad_x_taps, chan_start, total_channels),
            widen(grad_x_shift, chan_start, total_channels),
            grad_bc_taps,
            grad_bc_shift,
            widen(grad_dt_shift, head_start, total_heads),
            widen(grad_log_rate, head_start, total_heads),
            widen(grad_skip, head_start, total_heads),
            widen(grad_gain_local, chan_start, total_channels),
        ),
        ("dp", "tensor"),
    )
    grad_ng, grad_cx, grad_cxb, grad_cbc, grad_cbcb, grad_dtb, grad_alog, grad_dsk, grad_gg = (
        small_sums
    )
    return (
        out_acts,
        grad_acts,
        grad_ng,
        grad_w_zx,
        grad_w_bc,
        grad_w_dt,
        grad_w_out,
        grad_cx,
        grad_cxb,
        grad_cbc,
        grad_cbcb,
        grad_dtb,
        grad_alog,
        grad_dsk,
        grad_gg,
    )


def solution(mesh):
    in_specs = (
        P("dp", "tensor", None),
        P("dp", "tensor", None),
        P(),
        P("dp", None, "tensor"),
        P("dp", None),
        P("dp", "tensor"),
        P("dp", "tensor"),
        P(),
        P(),
        P(),
        P(),
        P(),
        P(),
        P(),
        P(),
    )
    out_specs = (
        P("dp", "tensor", None),
        P("dp", "tensor", None),
        P(),
        P("dp", None, "tensor"),
        P("dp", None),
        P("dp", "tensor"),
        P("dp", "tensor"),
        P(),
        P(),
        P(),
        P(),
        P(),
        P(),
        P(),
        P(),
    )
    return jax.shard_map(body, mesh=mesh, in_specs=in_specs, out_specs=out_specs, check_vma=False)
```

profile of v0, /device:TPU:0, one launch (start us, length us, event | category | flops | bytes accessed | tf_op | source)
XLA Modules:
  0.0 918.6 jit_solution(7278153467009917441)
XLA Ops:
  16.2 27.9 %all_gather.19 = bf16[1024,8]{0,1:T(8,128)(2,1)S(1)} all-gather(bf16[128,8]{0,1:T(8,128)(2,1)S(1)} %copy-done.49), channel_id=1, replica_groups=mesh['dp'=8,'tensor'=4] {'dp'}, dimensions={0}, use_global_device_ids=true | all-gather | bytes 18432 | tf_op jit(solution)/shard_map/all_gather | solution.py:123
  44.2 32.4 %all_gather.21 = bf16[1024,256]{1,0:T(8,128)(2,1)S(1)} all-gather(bf16[128,256]{1,0:T(8,128)(2,1)S(1)} %copy-done.20), channel_id=1, replica_groups=mesh['dp'=8,'tensor'=4] {'dp'}, dimensions={0}, use_global_device_ids=true | all-gather | bytes 589824 | tf_op jit(solution)/shard_map/all_gather | solution.py:122
  77.6 3.8 fusion.161
  86.3 15.2 %all-gather.8.cloned.1.call-done = bf16[1024,2,512]{2,0,1:T(8,128)(2,1)} async-done(((bf16[128,2,512]{2,0,1:T(8,128)(2,1)}), bf16[1024,2,512]{2,0,1:T(8,128)(2,1)}) %all-gather.8.cloned.1.call-update) | async-done | bytes 2097168 | tf_op jit(solution)/shard_map/all_gather | solution.py:121
  101.5 7.1 fusion.109
  109.1 3.2 copy-done.1
  112.3 4.7 fusion.123
  117.0 7.1 reshape.372
  124.1 6.9 copy.89
  130.9 4.0 compare_select_fusion.2
  137.4 87.5 %while.43 = (s32[]{:T(128)}, f32[8,64,128]{2,1,0:T(8,128)S(1)}, f32[8,256,8,64]{1,3,2,0:T(8,128)}, f32[8,8,64,128]{3,2,1,0:T(8,128)}, f32[8,256,8]{1,2,0:T(8,128...) while((s32[]{:T(128)}, f32[8,64,128]{2,1,0:T(8,128)S(1)}, ...), condition=%wide.region_4.5_spmd.clone.clone, body=%wide.region_1.4_spmd.clone.clone.sunk | while | flops 909711360 | bytes 5641051 | solution.py:56
  140.0 3.6 fusion.270
  150.9 3.6 fusion.270
  161.9 3.6 fusion.270
  172.9 3.6 fusion.270
  183.8 3.6 fusion.270
  194.7 3.6 fusion.270
  205.7 3.6 fusion.270
  216.6 3.6 fusion.270
  225.0 6.9 copy.101
  231.9 7.5 reshape.369
  239.4 7.6 multiply_reduce_fusion.8
  246.9 5.7 psum.84
  252.7 7.2 fusion.130
  260.0 7.4 fusion.96
  267.5 6.8 psum.85
  274.3 11.7 %multiply_reduce_fusion.3 = (f32[512]{0:T(512)}, f32[2048,512]{1,0:T(8,128)}, bf16[2048,1,512]{2,0,1:T(8,128)(2,1)}) fusion(f32[2048,512]{1,0:T(8,128)} %get-tuple-element.766, f32[2048,2,512]{2,0,1:T(8,128)} %copy-done.1, f32[2048]{0:T(1024)S(1)} %broadcast_multiply_fusion.8, f32[2048,512]{1,0:T(8,128)} %get-tuple-element.762, ...), kind=kLoop, calls=%fused_computation.161 | loop fusion | flops 30408192 | bytes 25196544 | tf_op jit(solution)/shard_map/transpose(jvp())/reduce_sum | solution.py:83
  286.0 7.1 reshape.370
  293.1 6.8 copy.94
  305.2 198.0 %while.42 = (s32[]{:T(128)}, f32[8]{0:T(128)}, f32[8,64,128]{2,1,0:T(8,128)S(1)}, f32[8,256,8,64]{1,3,2,0:T(8,128)}, f32[8,256,8]{1,2,0:T(8,128)}, /*index=5*/f3...) while((s32[]{:T(128)}, f32[8]{0:T(128)}, ...), condition=%wide.region_24.25_spmd.clone, body=%wide.region_10.0_spmd.clone.sunk | while | flops 2126610432 | bytes 15952340 | solution.py:56
  313.2 3.4 fusion.252
  326.8 2.8 fusion.257
  337.4 3.4 fusion.252
  351.6 2.8 fusion.257
  362.2 3.4 fusion.252
  376.4 2.8 fusion.257
  387.0 3.4 fusion.252
  401.2 2.8 fusion.257
  411.8 3.4 fusion.252
  426.0 2.8 fusion.257
  436.6 3.4 fusion.252
  450.8 2.8 fusion.257
  461.5 3.4 fusion.252
  475.6 2.8 fusion.257
  486.3 3.4 fusion.252
  500.4 2.8 fusion.257
  503.2 6.9 copy.104
  510.1 7.5 reshape.371
  517.7 11.5 %multiply_reduce_fusion.6 = (f32[512]{0:T(512)S(1)}, f32[512]{0:T(512)S(1)}, f32[512]{0:T(512)S(1)}, f32[512]{0:T(512)S(1)}, f32[512]{0:T(512)S(1)}, /*index=5*/f32[2048,512]{1,0:T(8,128)S(1)}) fusion(f32[2048,512]{1,0:T(8,128)} %copy-done, f32[2048,2,512]{2,0,1:T(8,128)} %copy-done.1, f32[2048,512]{1,0:T(8,128)} %get-tuple-element.766, ...), kind=kLoop, calls=%fused_computation.164 | loop fusion | flops 20968960 | bytes 25178112 | tf_op jit(solution)/shard_map/transpose(jvp())/reduce_sum | solution.py:19
  529.2 5.8 broadcast_multiply_fusion
  535.0 7.1 fusion.127
  542.2 8.2 fusion.107
  554.3 6.8 bitcast_add_fusion
  562.4 7.8 fusion.148
  572.1 3.2 multiply_reduce_fusion.12
  579.6 40.8 %all-reduce.21 = bf16[2048,256]{1,0:T(8,128)(2,1)S(1)} all-reduce(f32[2048,256]{1,0:T(8,128)S(1)} %pad_add_fusion.3), channel_id=1, replica_groups=mesh['dp'=8,'tensor'=4] {'tensor'}, use_global_device_ids=true, to_apply=%region_26.27 | all-reduce | flops 524288 | bytes 3145728 | tf_op jit(solution)/shard_map/psum | solution.py:195
  620.5 4.9 fusion.162
  628.7 8.8 reduce-scatter.11.cloned.1.call-done
  639.7 71.4 %reduce-scatter.9.cloned.1.call-done = f32[512,1024]{1,0:T(8,128)} async-done(((f32[2048,1024]{1,0:T(8,128)}), f32[512,1024]{1,0:T(8,128)}) %reduce-scatter.9.cloned.1.call-update) | async-done | bytes 2097168 | tf_op jit(solution)/shard_map/reduce_scatter | solution.py:206
  713.8 41.1 %all-reduce.19 = (f32[1024]{0:T(1024)}, f32[4,2048]{1,0:T(4,128)}, f32[2048]{0:T(1024)}, f32[4,256]{1,0:T(4,128)}, f32[256]{0:T(256)}, /*index=5*/f32[32]{0:T(128)}, f32[32]{0:T(128)}, f32[32]{0:T(128)}, f32[2048]{0:T(1024)}) all-reduce(f32[1024]{0:T(1024)S(1)} %get-tuple-element.689, ...), channel_id=1, replica_groups=mesh['dp'=8,'tensor'=4] {'dp','tensor'}, use_global_device_ids=true, to_apply=%region_29.30 | all-reduce | flops 14688 | bytes 117504 | tf_op jit(solution)/shard_map/psum | solution.py:225
  754.9 30.9 %reduce-scatter.7.cloned.1.call-done = f32[512,1024]{1,0:T(8,128)} async-done(((f32[2048,1024]{1,0:T(8,128)}), f32[512,1024]{1,0:T(8,128)}) %reduce-scatter.7.cloned.1.call-update) | async-done | bytes 2097168 | tf_op jit(solution)/shard_map/reduce_scatter | solution.py:159
  785.8 4.3 fusion.122
  790.0 54.2 %reduce-scatter.15.cloned.1.call-done = f32[128,8]{0,1:T(8,128)} async-done(((f32[1024,8]{0,1:T(8,128)}), f32[128,8]{0,1:T(8,128)}) %reduce-scatter.15.cloned.1.call-update) | async-done | bytes 4112 | tf_op jit(solution)/shard_map/reduce_scatter | solution.py:222
  844.3 67.1 %reduce-scatter.13.cloned.1.call-done = f32[128,256]{1,0:T(8,128)} async-done(((f32[1024,256]{1,0:T(8,128)}), f32[128,256]{1,0:T(8,128)}) %reduce-scatter.13.cloned.1.call-update) | async-done | bytes 131088 | tf_op jit(solution)/shard_map/reduce_scatter | solution.py:221
  (583 shorter events, 248.3 us)
Async XLA Ops:
  7.2 4.3 copy-start.14
  7.2 6.4 copy-start.52
  7.2 7.1 copy-start.55
  7.2 7.2 copy-start.56
  7.2 8.9 copy-start.48
  7.2 8.9 copy-start.49
  7.2 36.9 %copy-start.20 = (bf16[128,256]{1,0:T(8,128)(2,1)S(1)}, bf16[128,256]{1,0:T(8,128)(2,1)}, u32[]{:S(2)}) copy-start(bf16[128,256]{1,0:T(8,128)(2,1)} %param.23) | copy-start | bytes 196612
  7.3 70.3 %all-gather.6.cloned.1.call-start = ((), (), s32[]{:S(2)}) async-start(), calls=%async_computation.6 | async-start | bytes 5242880 | tf_op jit(solution)/shard_map/all_gather | solution.py:128
  8.9 7.3 copy-start.36
  8.9 7.3 copy-start.24
  11.4 90.1 %all-gather.8.cloned.1.call-start = ((), (), s32[]{:S(2)}) async-start(), calls=%async_computation.7 | async-start | bytes 2359296 | tf_op jit(solution)/shard_map/all_gather | solution.py:121
  12.2 240.5 %all-gather.12.cloned.1.call-start = ((), (), s32[]{:S(2)}) async-start(), calls=%async_computation.15 | async-start | bytes 5242880 | tf_op jit(solution)/shard_map/all_gather | solution.py:167
  13.0 247.0 %all-gather.10.cloned.1.call-start = ((), (), s32[]{:S(2)}) async-start(), calls=%async_computation.8 | async-start | bytes 1179648 | tf_op jit(solution)/shard_map/all_gather | solution.py:124
  13.6 613.3 %reduce-scatter.17.cloned.1.call-start = ((), (), s32[]{:S(2)}) async-start(), calls=%async_computation.14 | async-start | bytes 2359296 | tf_op jit(solution)/shard_map/reduce_scatter | solution.py:223
  15.2 259.0 %copy-start.26 = (f32[512]{0:T(512)}, f32[512]{0:T(512)S(1)}, u32[]{:S(2)}) copy-start(f32[512]{0:T(512)S(1)} %dynamic_slice.100) | copy-start | bytes 6148
  16.1 258.1 %copy-start.22 = (f32[512]{0:T(512)}, f32[512]{0:T(512)S(1)}, u32[]{:S(2)}) copy-start(f32[512]{0:T(512)S(1)} %mul.863) | copy-start | bytes 6148
  16.2 65.2 %copy-start.39 = (f32[1,256]{1,0:T(1,128)}, f32[1,256]{1,0:T(1,128)S(1)}, u32[]{:S(2)}) copy-start(f32[1,256]{1,0:T(1,128)S(1)} %get-tuple-element.793) | copy-start | bytes 3076
  16.2 65.2 %copy-start.41 = (f32[1,256]{1,0:T(1,128)}, f32[1,256]{1,0:T(1,128)S(1)}, u32[]{:S(2)}) copy-start(f32[1,256]{1,0:T(1,128)S(1)} %get-tuple-element.794) | copy-start | bytes 3076
  16.2 65.2 %copy-start.43 = (f32[1,256]{1,0:T(1,128)}, f32[1,256]{1,0:T(1,128)S(1)}, u32[]{:S(2)}) copy-start(f32[1,256]{1,0:T(1,128)S(1)} %get-tuple-element.795) | copy-start | bytes 3076
  16.2 65.2 %copy-start.45 = (f32[1,256]{1,0:T(1,128)}, f32[1,256]{1,0:T(1,128)S(1)}, u32[]{:S(2)}) copy-start(f32[1,256]{1,0:T(1,128)S(1)} %get-tuple-element.796) | copy-start | bytes 3076
  44.1 86.8 %copy-start.18 = (bf16[1024,8]{0,1:T(8,128)(2,1)}, bf16[1024,8]{0,1:T(8,128)(2,1)S(1)}, u32[]{:S(2)}) copy-start(bf16[1024,8]{0,1:T(8,128)(2,1)S(1)} %all_gather.19) | copy-start | bytes 49156
  44.2 37.3 %copy-start.51 = (f32[256]{0:T(256)S(1)}, f32[256]{0:T(256)}, u32[]{:S(2)}) copy-start(f32[256]{0:T(256)} %param.29) | copy-start | bytes 3076
  76.6 4.8 copy-start.10
  77.5 34.7 %copy-start.28 = (f32[1,512]{1,0:T(1,128)}, f32[1,512]{1,0:T(1,128)S(1)}, u32[]{:S(2)}) copy-start(f32[1,512]{1,0:T(1,128)S(1)} %get-tuple-element.787) | copy-start | bytes 6148
  77.5 34.7 %copy-start.30 = (f32[1,512]{1,0:T(1,128)}, f32[1,512]{1,0:T(1,128)S(1)}, u32[]{:S(2)}) copy-start(f32[1,512]{1,0:T(1,128)S(1)} %get-tuple-element.788) | copy-start | bytes 6148
  77.6 34.7 %copy-start.32 = (f32[1,512]{1,0:T(1,128)}, f32[1,512]{1,0:T(1,128)S(1)}, u32[]{:S(2)}) copy-start(f32[1,512]{1,0:T(1,128)S(1)} %get-tuple-element.789) | copy-start | bytes 6148
  77.6 34.7 %copy-start.34 = (f32[1,512]{1,0:T(1,128)}, f32[1,512]{1,0:T(1,128)S(1)}, u32[]{:S(2)}) copy-start(f32[1,512]{1,0:T(1,128)S(1)} %get-tuple-element.790) | copy-start | bytes 6148
  81.4 3.9 copy-start.5
  108.6 3.7 copy-start.1
  112.3 4.7 copy-start
  252.7 21.6 %copy-start.16 = (f32[2048]{0:T(1024)}, f32[2048]{0:T(1024)S(1)}, u32[]{:S(2)}) copy-start(f32[2048]{0:T(1024)S(1)} %get-tuple-element.792) | copy-start | bytes 24580
  260.0 377.4 %reduce-scatter.11.cloned.1.call-start = ((), (), s32[]{:S(2)}) async-start(), calls=%async_computation.11 | async-start | bytes 4718592 | tf_op jit(solution)/shard_map/reduce_scatter | solution.py:220
  510.1 7.5 copy-start.23
  517.6 11.6 %copy-start.29 = (f32[1,512]{1,0:T(1,128)S(1)}, f32[1,512]{1,0:T(1,128)}, u32[]{:S(2)}) copy-start(f32[1,512]{1,0:T(1,128)} %copy-done.28) | copy-start | bytes 6148
  517.6 11.6 %copy-start.31 = (f32[1,512]{1,0:T(1,128)S(1)}, f32[1,512]{1,0:T(1,128)}, u32[]{:S(2)}) copy-start(f32[1,512]{1,0:T(1,128)} %copy-done.30) | copy-start | bytes 6148
  517.6 11.6 %copy-start.33 = (f32[1,512]{1,0:T(1,128)S(1)}, f32[1,512]{1,0:T(1,128)}, u32[]{:S(2)}) copy-start(f32[1,512]{1,0:T(1,128)} %copy-done.32) | copy-start | bytes 6148
  517.6 11.6 %copy-start.35 = (f32[1,512]{1,0:T(1,128)S(1)}, f32[1,512]{1,0:T(1,128)}, u32[]{:S(2)}) copy-start(f32[1,512]{1,0:T(1,128)} %copy-done.34) | copy-start | bytes 6148
  535.0 7.2 copy-start.2
  550.4 160.6 %reduce-scatter.9.cloned.1.call-start = ((), (), s32[]{:S(2)}) async-start(), calls=%async_computation.10 | async-start | bytes 10485760 | tf_op jit(solution)/shard_map/reduce_scatter | solution.py:206
  551.5 1.6 copy-start.8
  551.5 2.2 copy-start.9
  551.5 2.8 copy-start.54
  561.2 1.2 copy-start.12
  561.2 1.2 copy-start.17
  561.2 1.2 copy-start.27
  561.2 224.6 %reduce-scatter.7.cloned.1.call-start = ((), (), s32[]{:S(2)}) async-start(), calls=%async_computation.9 | async-start | bytes 10485760 | tf_op jit(solution)/shard_map/reduce_scatter | solution.py:159
  570.2 1.6 copy-start.6
  570.2 1.9 copy-start.7
  570.2 274.0 %reduce-scatter.15.cloned.1.call-start = ((), (), s32[]{:S(2)}) async-start(), calls=%async_computation.13 | async-start | bytes 36864 | tf_op jit(solution)/shard_map/reduce_scatter | solution.py:222
  572.1 3.2 copy-start.40
  572.1 3.2 copy-start.42
  572.1 3.2 copy-start.44
  572.1 3.2 copy-start.46
  576.0 2.3 copy-start.3
  620.4 5.1 copy-start.11
  620.4 5.1 copy-start.47
  620.4 5.1 copy-start.50
  620.4 6.2 copy-start.38
  620.4 6.2 copy-start.53
  620.4 90.6 %copy-start.4 = (bf16[1,512,1024]{2,1,0:T(8,128)(2,1)S(1)}, bf16[1,512,1024]{2,1,0:T(8,128)(2,1)}, u32[]{:S(2)}) copy-start(bf16[1,512,1024]{2,1,0:T(8,128)(2,1)} %param.19) | copy-start | bytes 3145732
  620.5 90.6 %copy-start.21 = (f32[1024]{0:T(1024)S(1)}, f32[1024]{0:T(1024)}, u32[]{:S(2)}) copy-start(f32[1024]{0:T(1024)} %param.21) | copy-start | bytes 12292
  620.5 90.6 %copy-start.25 = (f32[512]{0:T(512)S(1)}, f32[512]{0:T(512)}, u32[]{:S(2)}) copy-start(f32[512]{0:T(512)} %copy-done.24) | copy-start | bytes 6148
  620.5 290.9 %reduce-scatter.13.cloned.1.call-start = ((), (), s32[]{:S(2)}) async-start(), calls=%async_computation.12 | async-start | bytes 1179648 | tf_op jit(solution)/shard_map/reduce_scatter | solution.py:221
  625.4 129.5 %copy-start.37 = (f32[512]{0:T(512)S(1)}, f32[512]{0:T(512)}, u32[]{:S(2)}) copy-start(f32[512]{0:T(512)} %copy-done.36) | copy-start | bytes 6148
  (3 other events, 2.8 us)
Sparse Core Ops, SparseCore 0:
  11.6 37.1 all-gather.5
  51.5 49.9 all-gather.7
  103.1 32.9 all-gather.11
  138.1 40.3 all-gather.9
  260.1 68.2 reduce-scatter.16
  550.6 86.8 reduce-scatter.10
  640.0 71.0 reduce-scatter.8
  713.6 72.0 reduce-scatter.6
  789.5 54.7 reduce-scatter.14
  848.1 63.1 reduce-scatter.12
where the time goes:
time: 926 us; the launch traced here: 919 us
  waiting for transfers between devices  249 us (27%)
  matrix products  235 us (25%)
  blocking collectives  155 us (17%)
  other arithmetic  140 us (15%)
  local copies, waits for them, and re-layouts  123 us (13%)
  between operations  15.3 us (2%)
    dot_general x24, matrix products, step_block(): jnp.einsum('ijh,jhp->ihp', weights, x_block, precision=FULL_PRECISION)  78.3 us
    reduce_scatter x1, waiting for transfers between devices, body(): lax.psum_scatter(from_zx + lax.dot_general(grad_dt_low, dt_full, CONTRACT...  71.4 us
    reduce_scatter x1, waiting for transfers between devices, body(): lax.psum_scatter(grad_bc_w, 'dp', scatter_dimension=0, tiled=True)  67.1 us
    reduce_scatter x1, waiting for transfers between devices, body(): lax.psum_scatter(grad_dt_w, 'dp', scatter_dimension=0, tiled=True)  54.2 us
    psum x1, blocking collectives, body(): lax.psum((grad_norm_gain, widen(grad_x_taps, chan_start, total_channels),...  41.1 us
    psum x1, blocking collectives, body(): grad_bc_in = lax.psum(grad_bc_part, 'tensor').astype(jnp.bfloat16)  40.8 us
    another operation x73, other arithmetic  39.1 us
    dot_general x32, matrix products, step_block(): jnp.einsum('in,hpn->ihp', c_block, state, precision=FULL_PRECISION)  35.8 us
  transfers between devices with their start and end apart: 10, of which 6 were waited for; matrix products, arithmetic and copies ran while one was open for 53% of the time, Pallas kernels for 0%

commit v1 on v0

--- a/solution.py
+++ b/solution.py
@@ -8,6 +8,44 @@
 FULL_PRECISION = lax.Precision.HIGHEST
 CONTRACT_LAST = (((1,), (1,)), ((), ()))
 CONTRACT_FIRST = (((0,), (0,)), ((), ()))
+
+
+def spread_the_steps_all(field_in):
+    d_next, block_now, met_up = (
+        jax.lax.axis_size("dp"),
+        jax.lax.axis_index("dp"),
+        field_in.shape[0],
+    )
+    rows = []
+    for hop_no, w in enumerate(field_in.shape):
+        rows.append(w * d_next if hop_no == 0 else w)
+    w2 = lax.dynamic_update_slice_in_dim(
+        jnp.zeros(rows, field_in.dtype), field_in, block_now * met_up, axis=0
+    )
+    vec_out = u_next = field_in
+    nth = 1
+    while nth < d_next // 2 + 1:
+        all_rows = []
+        hop_no = 0
+        while hop_no < d_next:
+            all_rows.append((hop_no, (hop_no + 1) % d_next))
+            hop_no += 1
+        vec_out = jax.lax.ppermute(vec_out, "dp", perm=all_rows)
+        w2 = lax.dynamic_update_slice_in_dim(
+            w2, vec_out, (block_now - nth) % d_next * met_up, axis=0
+        )
+        if 2 * nth < d_next:
+            arrivals = []
+            hop_no = 0
+            while hop_no < d_next:
+                arrivals.append((hop_no, (hop_no - 1) % d_next))
+                hop_no += 1
+            u_next = jax.lax.ppermute(u_next, "dp", arrivals)
+            w2 = lax.dynamic_update_slice_in_dim(
+                w2, u_next, (block_now + nth) % d_next * met_up, axis=0
+            )
+        nth = nth + 1
+    return w2
 
 
 def causal_conv(values, conv_taps):
@@ -120,7 +158,7 @@
     zx_full, bc_full, dt_full, out_full = (
         lax.all_gather(w_zx, "dp", axis=0, tiled=True),
         lax.all_gather(w_bc, "dp", axis=0, tiled=True),
-        lax.all_gather(w_dt, "dp", axis=0, tiled=True),
+        spread_the_steps_all(w_dt),
         lax.all_gather(w_out, "dp", axis=0, tiled=True),
     )
     acts_row = acts[0].astype(jnp.float32)

time: 926 us -> 925 us (level)
  blocking collectives: 155 us -> 126 us
  starting transfers between devices: 0.66 us -> 16.4 us
    all_gather x1 -> x0, blocking collectives: 27.9 us -> none  [body(): lax.all_gather(w_dt, 'dp', axis=0, tiled=True)]
    ppermute x0 -> x7, starting transfers between devices: none -> 15.4 us  [the longest x3 15.4 us: spread_the_steps_all(): u_next = jax.lax.ppermute(u_next, 'dp', arrivals)]
    ppermute x0 -> x7, waiting for transfers between devices: none -> 13.9 us  [the longest x4 12.6 us: spread_the_steps_all(): vec_out = jax.lax.ppermute(vec_out, 'dp', perm=all_rows)]
    unnamed x119 -> x117, local copies, waits for them, and re-layouts: 28.6 us -> 27.7 us
  transfers between devices with their start and end apart: 10 -> 17, of which waited for: 6 -> 10; matrix products, arithmetic and copies ran while one was open for 53% -> 53% of each run, Pallas kernels for 0% -> 0%
where the time goes in v1:
time: 925 us; the launch traced here: 918 us
  waiting for transfers between devices  257 us (28%)
  matrix products  240 us (26%)
  other arithmetic  140 us (15%)
  blocking collectives  126 us (14%)
  local copies, waits for them, and re-layouts  122 us (13%)
  starting transfers between devices  16.4 us (2%)
  between operations  15.6 us (2%)
    dot_general x24, matrix products, step_block(): jnp.einsum('ijh,jhp->ihp', weights, x_block, precision=FULL_PRECISION)  78.3 us
    reduce_scatter x1, waiting for transfers between devices, body(): lax.psum_scatter(from_zx + lax.dot_general(grad_dt_low, dt_full, CONTRACT...  71.4 us
    reduce_scatter x1, waiting for transfers between devices, body(): lax.psum_scatter(grad_bc_w, 'dp', scatter_dimension=0, tiled=True)  67.1 us
    reduce_scatter x1, waiting for transfers between devices, body(): lax.psum_scatter(grad_dt_w, 'dp', scatter_dimension=0, tiled=True)  53.5 us
    psum x1, blocking collectives, body(): lax.psum((grad_norm_gain, widen(grad_x_taps, chan_start, total_channels),...  41.1 us
    psum x1, blocking collectives, body(): grad_bc_in = lax.psum(grad_bc_part, 'tensor').astype(jnp.bfloat16)  40.6 us
    another operation x73, other arithmetic  39.1 us
    dot_general x32, matrix products, step_block(): jnp.einsum('in,hpn->ihp', c_block, state, precision=FULL_PRECISION)  35.8 us
  transfers between devices with their start and end apart: 17, of which 10 were waited for; matrix products, arithmetic and copies ran while one was open for 53% of the time, Pallas kernels for 0%

profile of v1, /device:TPU:0, one launch (start us, length us, event | category | flops | bytes accessed | tf_op | source)
XLA Modules:
  0.0 917.9 jit_solution(10180058066860977953)
XLA Ops:
  13.0 6.1 collective-permute-start.1
  20.1 31.6 %all_gather.17 = bf16[1024,256]{1,0:T(8,128)(2,1)S(1)} all-gather(bf16[128,256]{1,0:T(8,128)(2,1)S(1)} %copy-done.20), channel_id=1, replica_groups=mesh['dp'=8,'tensor'=4] {'dp'}, dimensions={0}, use_global_device_ids=true | all-gather | bytes 589824 | tf_op jit(solution)/shard_map/all_gather | solution.py:160
  54.7 4.4 collective-permute-start.3
  60.4 5.0 collective-permute-start.5
  65.4 6.3 collective-permute-done.4
  71.7 6.3 collective-permute-done.6
  78.0 3.6 fusion.162
  86.5 14.2 %all-gather.8.cloned.1.call-done = bf16[1024,2,512]{2,0,1:T(8,128)(2,1)} async-done(((bf16[128,2,512]{2,0,1:T(8,128)(2,1)}), bf16[1024,2,512]{2,0,1:T(8,128)(2,1)}) %all-gather.8.cloned.1.call-update) | async-done | bytes 2097168 | tf_op jit(solution)/shard_map/all_gather | solution.py:159
  100.7 7.1 fusion.109
  108.2 3.2 copy-done.1
  111.4 4.6 fusion.124
  116.1 7.1 reshape.372
  123.2 6.9 copy.89
  130.1 4.0 compare_select_fusion.2
  136.6 87.6 %while.43 = (s32[]{:T(128)}, f32[8,64,128]{2,1,0:T(8,128)S(1)}, f32[8,256,8,64]{1,3,2,0:T(8,128)}, f32[8,8,64,128]{3,2,1,0:T(8,128)}, f32[8,256,8]{1,2,0:T(8,128...) while((s32[]{:T(128)}, f32[8,64,128]{2,1,0:T(8,128)S(1)}, ...), condition=%wide.region_4.5_spmd.clone.clone, body=%wide.region_1.4_spmd.clone.clone.sunk | while | flops 909711360 | bytes 5641051 | solution.py:94
  139.1 3.6 fusion.271
  150.1 3.6 fusion.271
  161.1 3.6 fusion.271
  172.1 3.6 fusion.271
  183.0 3.6 fusion.271
  193.9 3.6 fusion.271
  204.9 3.6 fusion.271
  215.8 3.6 fusion.271
  224.2 6.9 copy.101
  231.1 7.5 reshape.369
  238.6 7.5 multiply_reduce_fusion.8
  246.1 5.7 psum.84
  251.9 7.2 fusion.131
  259.2 7.4 fusion.96
  266.6 6.7 psum.85
  273.4 11.7 %multiply_reduce_fusion.3 = (f32[512]{0:T(512)}, f32[2048,512]{1,0:T(8,128)}, bf16[2048,1,512]{2,0,1:T(8,128)(2,1)}) fusion(f32[2048,512]{1,0:T(8,128)} %get-tuple-element.766, f32[2048,2,512]{2,0,1:T(8,128)} %copy-done.1, f32[2048]{0:T(1024)S(1)} %broadcast_multiply_fusion.8, f32[2048,512]{1,0:T(8,128)} %get-tuple-element.762, ...), kind=kLoop, calls=%fused_computation.161 | loop fusion | flops 30408192 | bytes 25196544 | tf_op jit(solution)/shard_map/transpose(jvp())/reduce_sum | solution.py:121
  285.1 7.1 reshape.370
  292.2 6.8 copy.94
  304.3 198.0 %while.42 = (s32[]{:T(128)}, f32[8]{0:T(128)}, f32[8,64,128]{2,1,0:T(8,128)S(1)}, f32[8,256,8,64]{1,3,2,0:T(8,128)}, f32[8,256,8]{1,2,0:T(8,128)}, /*index=5*/f3...) while((s32[]{:T(128)}, f32[8]{0:T(128)}, ...), condition=%wide.region_24.25_spmd.clone, body=%wide.region_10.24_spmd.clone.sunk | while | flops 2126610432 | bytes 15952340 | solution.py:94
  312.4 3.4 fusion.253
  336.5 3.4 fusion.253
  361.3 3.4 fusion.253
  386.1 3.4 fusion.253
  400.3 2.8 fusion.258
  410.9 3.4 fusion.253
  425.1 2.8 fusion.258
  435.8 3.4 fusion.253
  460.6 3.4 fusion.253
  485.4 3.4 fusion.253
  502.3 6.9 copy.104
  509.2 7.5 reshape.371
  516.8 11.6 %multiply_reduce_fusion.6 = (f32[512]{0:T(512)S(1)}, f32[512]{0:T(512)S(1)}, f32[512]{0:T(512)S(1)}, f32[512]{0:T(512)S(1)}, f32[512]{0:T(512)S(1)}, /*index=5*/f32[2048,512]{1,0:T(8,128)S(1)}) fusion(f32[2048,512]{1,0:T(8,128)} %copy-done, f32[2048,2,512]{2,0,1:T(8,128)} %copy-done.1, f32[2048,512]{1,0:T(8,128)} %get-tuple-element.766, ...), kind=kLoop, calls=%fused_computation.164 | loop fusion | flops 20968960 | bytes 25178112 | tf_op jit(solution)/shard_map/transpose(jvp())/reduce_sum | solution.py:57
  528.4 5.7 broadcast_multiply_fusion
  534.1 7.1 fusion.128
  541.3 8.3 fusion.107
  551.2 6.9 fusion.115
  558.1 4.5 bitcast_add_fusion
  563.9 7.8 fusion.149
  573.7 3.2 multiply_reduce_fusion.12
  581.0 40.6 %all-reduce.21 = bf16[2048,256]{1,0:T(8,128)(2,1)S(1)} all-reduce(f32[2048,256]{1,0:T(8,128)S(1)} %pad_add_fusion.3), channel_id=1, replica_groups=mesh['dp'=8,'tensor'=4] {'tensor'}, use_global_device_ids=true, to_apply=%region_26.27 | all-reduce | flops 524288 | bytes 3145728 | tf_op jit(solution)/shard_map/psum | solution.py:233
  622.1 4.8 fusion.163
  630.1 6.5 reduce-scatter.11.cloned.1.call-done
  638.8 71.4 %reduce-scatter.9.cloned.1.call-done = f32[512,1024]{1,0:T(8,128)} async-done(((f32[2048,1024]{1,0:T(8,128)}), f32[512,1024]{1,0:T(8,128)}) %reduce-scatter.9.cloned.1.call-update) | async-done | bytes 2097168 | tf_op jit(solution)/shard_map/reduce_scatter | solution.py:244
  710.3 4.0 fusion.119
  714.3 41.1 %all-reduce.19 = (f32[1024]{0:T(1024)}, f32[4,2048]{1,0:T(4,128)}, f32[2048]{0:T(1024)}, f32[4,256]{1,0:T(4,128)}, f32[256]{0:T(256)}, /*index=5*/f32[32]{0:T(128)}, f32[32]{0:T(128)}, f32[32]{0:T(128)}, f32[2048]{0:T(1024)}) all-reduce(f32[1024]{0:T(1024)S(1)} %get-tuple-element.683, ...), channel_id=1, replica_groups=mesh['dp'=8,'tensor'=4] {'dp','tensor'}, use_global_device_ids=true, to_apply=%region_29.30 | all-reduce | flops 14688 | bytes 117504 | tf_op jit(solution)/shard_map/psum | solution.py:263
  755.4 29.5 %reduce-scatter.7.cloned.1.call-done = f32[512,1024]{1,0:T(8,128)} async-done(((f32[2048,1024]{1,0:T(8,128)}), f32[512,1024]{1,0:T(8,128)}) %reduce-scatter.7.cloned.1.call-update) | async-done | bytes 2097168 | tf_op jit(solution)/shard_map/reduce_scatter | solution.py:197
  785.0 5.0 fusion.123
  790.0 53.5 %reduce-scatter.15.cloned.1.call-done = f32[128,8]{0,1:T(8,128)} async-done(((f32[1024,8]{0,1:T(8,128)}), f32[128,8]{0,1:T(8,128)}) %reduce-scatter.15.cloned.1.call-update) | async-done | bytes 4112 | tf_op jit(solution)/shard_map/reduce_scatter | solution.py:260
  843.5 67.1 %reduce-scatter.13.cloned.1.call-done = f32[128,256]{1,0:T(8,128)} async-done(((f32[1024,256]{1,0:T(8,128)}), f32[128,256]{1,0:T(8,128)}) %reduce-scatter.13.cloned.1.call-update) | async-done | bytes 131088 | tf_op jit(solution)/shard_map/reduce_scatter | solution.py:259
  (603 shorter events, 261.4 us)
Async XLA Ops:
  7.2 4.3 copy-start.14
  7.2 5.8 copy-start.49
  7.2 12.1 %copy-start.52 = (f32[32]{0:T(128)S(1)}, f32[32]{0:T(128)}, u32[]{:S(2)}) copy-start(f32[32]{0:T(128)} %param.31) | copy-start | bytes 388
  7.2 12.8 %copy-start.48 = (f32[4,256]{1,0:T(4,128)S(1)}, f32[4,256]{1,0:T(4,128)}, u32[]{:S(2)}) copy-start(f32[4,256]{1,0:T(4,128)} %param.28) | copy-start | bytes 12292
  7.2 12.8 %copy-start.20 = (bf16[128,256]{1,0:T(8,128)(2,1)S(1)}, bf16[128,256]{1,0:T(8,128)(2,1)}, u32[]{:S(2)}) copy-start(bf16[128,256]{1,0:T(8,128)(2,1)} %param.23) | copy-start | bytes 196612
  7.2 45.6 %copy-start.54 = (f32[32]{0:T(128)S(1)}, f32[32]{0:T(128)}, u32[]{:S(2)}) copy-start(f32[32]{0:T(128)} %param.30) | copy-start | bytes 388
  7.2 45.7 %copy-start.55 = (f32[32]{0:T(128)S(1)}, f32[32]{0:T(128)}, u32[]{:S(2)}) copy-start(f32[32]{0:T(128)} %param.32) | copy-start | bytes 388
  7.3 70.7 %all-gather.6.cloned.1.call-start = ((), (), s32[]{:S(2)}) async-start(), calls=%async_computation.6 | async-start | bytes 5242880 | tf_op jit(solution)/shard_map/all_gather | solution.py:166
  8.9 11.1 %copy-start.36 = (f32[512]{0:T(512)}, f32[512]{0:T(512)S(1)}, u32[]{:S(2)}) copy-start(f32[512]{0:T(512)S(1)} %fusion.125) | copy-start | bytes 6148
  8.9 11.1 %copy-start.24 = (f32[512]{0:T(512)}, f32[512]{0:T(512)S(1)}, u32[]{:S(2)}) copy-start(f32[512]{0:T(512)S(1)} %fusion.145) | copy-start | bytes 6148
  11.4 89.2 %all-gather.8.cloned.1.call-start = ((), (), s32[]{:S(2)}) async-start(), calls=%async_computation.7 | async-start | bytes 2359296 | tf_op jit(solution)/shard_map/all_gather | solution.py:159
  12.2 239.6 %all-gather.12.cloned.1.call-start = ((), (), s32[]{:S(2)}) async-start(), calls=%async_computation.15 | async-start | bytes 5242880 | tf_op jit(solution)/shard_map/all_gather | solution.py:205
  13.0 246.2 %all-gather.10.cloned.1.call-start = ((), (), s32[]{:S(2)}) async-start(), calls=%async_computation.8 | async-start | bytes 1179648 | tf_op jit(solution)/shard_map/all_gather | solution.py:162
  13.0 41.6 %collective-permute-start.1 = (bf16[128,8]{0,1:T(8,128)(2,1)S(1)}, bf16[128,8]{0,1:T(8,128)(2,1)S(1)}, u32[]{:S(2)}, u32[]{:S(2)}) collective-permute-start(bf16[128,8]{0,1:T(8,128)(2,1)S(1)} %copy-done.49), channel_id=1, source_target_pairs={{0,28},{4,0},{8,4},{12,8},{16,12},{20,16},{24,20},{28,24},{1,29},{... | collective-permute-start | bytes 6152 | tf_op jit(solution)/shard_map/ppermute | solution.py:43
  19.1 39.9 %collective-permute-start = (bf16[128,8]{0,1:T(8,128)(2,1)S(1)}, bf16[128,8]{0,1:T(8,128)(2,1)S(1)}, u32[]{:S(2)}, u32[]{:S(2)}) collective-permute-start(bf16[128,8]{0,1:T(8,128)(2,1)S(1)} %copy-done.49), channel_id=1, source_target_pairs={{0,4},{4,8},{8,12},{12,16},{16,20},{20,24},{24,28},{28,0},{1,5},{5... | collective-permute-start | bytes 6152 | tf_op jit(solution)/shard_map/ppermute | solution.py:33
  19.2 609.2 %reduce-scatter.17.cloned.1.call-start = ((), (), s32[]{:S(2)}) async-start(), calls=%async_computation.14 | async-start | bytes 2359296 | tf_op jit(solution)/shard_map/reduce_scatter | solution.py:261
  20.0 61.6 %copy-start.39 = (f32[1,256]{1,0:T(1,128)}, f32[1,256]{1,0:T(1,128)S(1)}, u32[]{:S(2)}) copy-start(f32[1,256]{1,0:T(1,128)S(1)} %get-tuple-element.793) | copy-start | bytes 3076
  20.0 61.6 %copy-start.41 = (f32[1,256]{1,0:T(1,128)}, f32[1,256]{1,0:T(1,128)S(1)}, u32[]{:S(2)}) copy-start(f32[1,256]{1,0:T(1,128)S(1)} %get-tuple-element.794) | copy-start | bytes 3076
  20.0 61.6 %copy-start.43 = (f32[1,256]{1,0:T(1,128)}, f32[1,256]{1,0:T(1,128)S(1)}, u32[]{:S(2)}) copy-start(f32[1,256]{1,0:T(1,128)S(1)} %get-tuple-element.795) | copy-start | bytes 3076
  20.1 61.6 %copy-start.45 = (f32[1,256]{1,0:T(1,128)}, f32[1,256]{1,0:T(1,128)S(1)}, u32[]{:S(2)}) copy-start(f32[1,256]{1,0:T(1,128)S(1)} %get-tuple-element.796) | copy-start | bytes 3076
  20.1 61.6 %copy-start.51 = (f32[256]{0:T(256)S(1)}, f32[256]{0:T(256)}, u32[]{:S(2)}) copy-start(f32[256]{0:T(256)} %param.29) | copy-start | bytes 3076
  51.7 29.9 %copy-start.10 = (bf16[1024,256]{1,0:T(8,128)(2,1)}, bf16[1024,256]{1,0:T(8,128)(2,1)S(1)}, u32[]{:S(2)}) copy-start(bf16[1024,256]{1,0:T(8,128)(2,1)S(1)} %all_gather.17) | copy-start | bytes 1572868
  52.7 58.7 %copy-start.28 = (f32[1,512]{1,0:T(1,128)}, f32[1,512]{1,0:T(1,128)S(1)}, u32[]{:S(2)}) copy-start(f32[1,512]{1,0:T(1,128)S(1)} %get-tuple-element.787) | copy-start | bytes 6148
  52.7 58.7 %copy-start.30 = (f32[1,512]{1,0:T(1,128)}, f32[1,512]{1,0:T(1,128)S(1)}, u32[]{:S(2)}) copy-start(f32[1,512]{1,0:T(1,128)S(1)} %get-tuple-element.788) | copy-start | bytes 6148
  52.7 58.7 %copy-start.32 = (f32[1,512]{1,0:T(1,128)}, f32[1,512]{1,0:T(1,128)S(1)}, u32[]{:S(2)}) copy-start(f32[1,512]{1,0:T(1,128)S(1)} %get-tuple-element.789) | copy-start | bytes 6148
  52.8 58.7 %copy-start.34 = (f32[1,512]{1,0:T(1,128)}, f32[1,512]{1,0:T(1,128)S(1)}, u32[]{:S(2)}) copy-start(f32[1,512]{1,0:T(1,128)S(1)} %get-tuple-element.790) | copy-start | bytes 6148
  53.8 219.6 %copy-start.26 = (f32[512]{0:T(512)}, f32[512]{0:T(512)S(1)}, u32[]{:S(2)}) copy-start(f32[512]{0:T(512)S(1)} %dynamic_slice.100) | copy-start | bytes 6148
  54.7 218.7 %copy-start.22 = (f32[512]{0:T(512)}, f32[512]{0:T(512)S(1)}, u32[]{:S(2)}) copy-start(f32[512]{0:T(512)S(1)} %mul.895) | copy-start | bytes 6148
  54.7 5.7 collective-permute-start.3
  59.1 6.3 collective-permute-start.2
  60.4 11.3 %collective-permute-start.5 = (bf16[128,8]{0,1:T(8,128)(2,1)S(1)}, bf16[128,8]{0,1:T(8,128)(2,1)S(1)}, u32[]{:S(2)}, u32[]{:S(2)}) collective-permute-start(bf16[128,8]{0,1:T(8,128)(2,1)S(1)} %collective-permute-done.3), channel_id=1, source_target_pairs={{0,28},{4,0},{8,4},{12,8},{16,12},{20,16},{24,20},{28,24},{1,29},{... | collective-permute-start | bytes 6152 | tf_op jit(solution)/shard_map/ppermute | solution.py:43
  65.4 6.3 collective-permute-start.4
  71.7 6.3 collective-permute-start.6
  78.0 52.1 %copy-start.18 = (bf16[1024,8]{0,1:T(8,128)(2,1)}, bf16[1024,8]{0,1:T(8,128)(2,1)S(1)}, u32[]{:S(2)}) copy-start(bf16[1024,8]{0,1:T(8,128)(2,1)S(1)} %constant_dynamic-update-slice_fusion) | copy-start | bytes 49156
  81.6 3.9 copy-start.6
  107.8 3.7 copy-start.1
  111.4 4.7 copy-start
  251.9 21.5 %copy-start.16 = (f32[2048]{0:T(1024)}, f32[2048]{0:T(1024)S(1)}, u32[]{:S(2)}) copy-start(f32[2048]{0:T(1024)S(1)} %get-tuple-element.792) | copy-start | bytes 24580
  259.1 377.4 %reduce-scatter.11.cloned.1.call-start = ((), (), s32[]{:S(2)}) async-start(), calls=%async_computation.11 | async-start | bytes 4718592 | tf_op jit(solution)/shard_map/reduce_scatter | solution.py:258
  509.2 7.5 copy-start.23
  516.8 11.6 %copy-start.29 = (f32[1,512]{1,0:T(1,128)S(1)}, f32[1,512]{1,0:T(1,128)}, u32[]{:S(2)}) copy-start(f32[1,512]{1,0:T(1,128)} %copy-done.28) | copy-start | bytes 6148
  516.8 11.6 %copy-start.31 = (f32[1,512]{1,0:T(1,128)S(1)}, f32[1,512]{1,0:T(1,128)}, u32[]{:S(2)}) copy-start(f32[1,512]{1,0:T(1,128)} %copy-done.30) | copy-start | bytes 6148
  516.8 11.6 %copy-start.33 = (f32[1,512]{1,0:T(1,128)S(1)}, f32[1,512]{1,0:T(1,128)}, u32[]{:S(2)}) copy-start(f32[1,512]{1,0:T(1,128)} %copy-done.32) | copy-start | bytes 6148
  516.8 11.6 %copy-start.35 = (f32[1,512]{1,0:T(1,128)S(1)}, f32[1,512]{1,0:T(1,128)}, u32[]{:S(2)}) copy-start(f32[1,512]{1,0:T(1,128)} %copy-done.34) | copy-start | bytes 6148
  534.1 7.2 copy-start.2
  549.6 160.7 %reduce-scatter.9.cloned.1.call-start = ((), (), s32[]{:S(2)}) async-start(), calls=%async_computation.10 | async-start | bytes 10485760 | tf_op jit(solution)/shard_map/reduce_scatter | solution.py:244
  551.2 6.9 copy-start.19
  562.7 222.3 %reduce-scatter.7.cloned.1.call-start = ((), (), s32[]{:S(2)}) async-start(), calls=%async_computation.9 | async-start | bytes 10485760 | tf_op jit(solution)/shard_map/reduce_scatter | solution.py:197
  571.7 271.8 %reduce-scatter.15.cloned.1.call-start = ((), (), s32[]{:S(2)}) async-start(), calls=%async_computation.13 | async-start | bytes 36864 | tf_op jit(solution)/shard_map/reduce_scatter | solution.py:260
  573.7 3.2 copy-start.40
  573.7 3.2 copy-start.42
  573.7 3.2 copy-start.44
  573.7 3.2 copy-start.46
  621.6 5.3 copy-start.11
  621.7 5.3 copy-start.47
  621.7 5.4 copy-start.50
  621.7 6.5 copy-start.38
  621.7 6.5 copy-start.53
  621.7 88.6 %copy-start.4 = (bf16[1,512,1024]{2,1,0:T(8,128)(2,1)S(1)}, bf16[1,512,1024]{2,1,0:T(8,128)(2,1)}, u32[]{:S(2)}) copy-start(bf16[1,512,1024]{2,1,0:T(8,128)(2,1)} %param.19) | copy-start | bytes 3145732
  621.7 88.5 %copy-start.21 = (f32[1024]{0:T(1024)S(1)}, f32[1024]{0:T(1024)}, u32[]{:S(2)}) copy-start(f32[1024]{0:T(1024)} %param.21) | copy-start | bytes 12292
  621.7 88.5 %copy-start.25 = (f32[512]{0:T(512)S(1)}, f32[512]{0:T(512)}, u32[]{:S(2)}) copy-start(f32[512]{0:T(512)} %copy-done.24) | copy-start | bytes 6148
  621.7 288.9 %reduce-scatter.13.cloned.1.call-start = ((), (), s32[]{:S(2)}) async-start(), calls=%async_computation.12 | async-start | bytes 1179648 | tf_op jit(solution)/shard_map/reduce_scatter | solution.py:259
  626.9 128.5 %copy-start.37 = (f32[512]{0:T(512)S(1)}, f32[512]{0:T(512)}, u32[]{:S(2)}) copy-start(f32[512]{0:T(512)} %copy-done.36) | copy-start | bytes 6148
  710.3 74.7 %copy-start.5 = (f32[512,1024]{1,0:T(8,128)S(1)}, f32[512,1024]{1,0:T(8,128)}, u32[]{:S(2)}) copy-start(f32[512,1024]{1,0:T(8,128)} %reduce-scatter.9.cloned.1.call-done) | copy-start | bytes 6291460
  (9 other events, 12.9 us)
Sparse Core Ops, SparseCore 0:
  11.6 37.1 all-gather.5
  51.5 49.0 all-gather.7
  102.2 32.9 all-gather.11
  137.2 40.3 all-gather.9
  259.3 68.0 reduce-scatter.16
  549.7 86.8 reduce-scatter.10
  639.2 71.0 reduce-scatter.8
  712.8 72.1 reduce-scatter.6
  788.7 54.7 reduce-scatter.14
  847.3 63.2 reduce-scatter.12
